TPU v7x, 512 devices: a 8x2x16 block of a 8x8x16 slice. The times are simulated.
512 devices in a mesh: groups: 2 (over y), seq: 16 (over z), fsdp: 8 (over x), sub: 2 (over core).
Axes of the slice: x: 8, y: 2, z: 16, core: 2. Of those that a mesh axis runs over, the one named last changes fastest.
The devices are a block of a 8x8x16 slice.
Arguments:
- tokens: bfloat16 [8192, 8192], P(('groups', 'seq')), parts along dimension 0, may hold values from -400 to 400
- norm_gain: float32 [8192], replicated, may hold values from 0.1 to 1.9
- w_query: bfloat16 [32, 16, 8192], P(('seq', 'sub'), 'fsdp'), may hold values from -0.0625 to 0.0625
- w_key: bfloat16 [32, 16, 8192], P(('seq', 'sub'), 'fsdp'), may hold values from -0.0625 to 0.0625
- w_value: bfloat16 [32, 128, 8192], P(('seq', 'sub'), 'fsdp'), may hold values from -5 to 5
- head_gain: float32 [128], replicated, may hold values from 0.1 to 1.9
- w_out: bfloat16 [32, 128, 8192], P('seq', None, ('fsdp', 'sub')), may hold values from -0.09375 to 0.09375
Outputs:
- mixed: bfloat16 [8192, 8192], P(('groups', 'seq'), ('fsdp', 'sub')), parts along dimension 0
There are 2 independent parts, one for each index of `groups`. A program takes and returns all parts, laid end to end along the dimension named above; an argument that names none is the same for every part. Nothing has to cross between parts.
All inputs are finite; a program needn't handle non-finite values.
Results may differ from a plain program's by a relative error of at most 0.0084.
Values may be sent and summed in bfloat16 or wider, within the bound.
A program may use at most 64 MiB of HBM per device.

v0:
```python
import math
import jax
import jax.numpy as jnp
import numpy as np
from jax import lax
from jax.sharding import PartitionSpec as P

BLOCK = 512


def laid_out(pieces, dim):
    pieces = jnp.moveaxis(pieces, 0, dim)
    dims = pieces.shape
    return pieces.reshape(*dims[:dim], dims[dim] * dims[dim + 1], *dims[dim + 2 :])


def copy_for_each(array, axis):
    copies = jnp.broadcast_to(array, (lax.axis_size(axis), *array.shape))
    return lax.all_to_all(copies, axis, split_axis=0, concat_axis=0, tiled=True)


def gathered_copies(array, axis, dim):
    return laid_out(copy_for_each(array, axis), dim)


def taylor_first(vectors):
    feature_count = vectors.shape[0]
    first_row, second_row = np.triu_indices(feature_count, 1)
    cross_terms = vectors[first_row] * vectors[second_row] / 4.0
    squares = vectors * vectors / (4.0 * math.sqrt(2.0))
    leading = jnp.ones((1,) + vectors.shape[1:], jnp.float32)
    return jnp.concatenate([leading, vectors / 2.0, cross_terms, squares], 0)


def head_norm(numerator, head_gain, channel_axis):
    widened = numerator.astype(jnp.float32)
    meansq = jnp.mean(widened * widened, axis=channel_axis, keepdims=True)
    gain_shape = tuple((-1 if axis_pos == channel_axis else 1 for axis_pos in range(widened.ndim)))
    return (widened * lax.rsqrt(meansq + 1e-06) * head_gain.reshape(gain_shape)).astype(
        jnp.bfloat16
    )


def attend(queries, key_vectors, values_local):
    length = queries.shape[1]
    nblocks = length // BLOCK
    channels = values_local.shape[0]
    query_feats = taylor_first(queries.astype(jnp.float32)).astype(jnp.bfloat16)
    key_feats = taylor_first(key_vectors.astype(jnp.float32)).astype(jnp.bfloat16)
    taylor_width = query_feats.shape[0]
    contrib = jnp.einsum(
        "fbj,ebj->bfe",
        key_feats.reshape(taylor_width, nblocks, BLOCK),
        values_local.reshape(channels, nblocks, BLOCK),
        preferred_element_type=jnp.float32,
    )
    prefix = jnp.concatenate([jnp.zeros_like(contrib[:1]), jnp.cumsum(contrib[:-1], axis=0)], 0)
    prior_state = prefix.astype(jnp.bfloat16)
    carried = jnp.einsum(
        "bfe,fbt->bet",
        prior_state,
        query_feats.reshape(taylor_width, nblocks, BLOCK),
        preferred_element_type=jnp.float32,
    )
    earlier = lax.broadcasted_iota(jnp.int32, (BLOCK, BLOCK), 0)
    column_pos = lax.broadcasted_iota(jnp.int32, (BLOCK, BLOCK), 1)
    causal = earlier <= column_pos

    def one_block(block_index):
        offset = block_index * BLOCK
        query_block = lax.dynamic_slice_in_dim(queries, offset, BLOCK, 1)
        key_block = lax.dynamic_slice_in_dim(key_vectors, offset, BLOCK, 1)
        value_block = lax.dynamic_slice_in_dim(values_local, offset, BLOCK, 1)
        scores = jnp.einsum("fj,ft->jt", key_block, query_block, preferred_element_type=jnp.float32)
        kernel = 1.0 + scores / 4.0 + scores * scores / 32.0
        weight = jnp.where(causal, kernel, 0.0).astype(jnp.bfloat16)
        return jnp.einsum("ej,jt->et", value_block, weight, preferred_element_type=jnp.float32)

    local_part = lax.map(one_block, jnp.arange(nblocks, dtype=jnp.int32))
    numerator = (local_part + carried).astype(jnp.bfloat16)
    return jnp.transpose(numerator, (1, 0, 2)).reshape(channels, length)


def per_device(tokens, norm_gain, w_query, w_key, w_value, head_gain, w_out):
    feat_dev = w_query.shape[1]
    inputs = tokens.astype(jnp.float32)
    meansq = jnp.mean(inputs * inputs, axis=1, keepdims=True)
    normed = (inputs * lax.rsqrt(meansq + 1e-05) * norm_gain).astype(jnp.bfloat16)
    stacked = jnp.concatenate([w_query, w_key, w_value], 1)
    head_weights = lax.all_gather(stacked, "seq", axis=0, tiled=True)
    projected = jnp.einsum(
        "hcd,td->hct", head_weights, normed, preferred_element_type=jnp.float32
    ).astype(jnp.bfloat16)
    by_head = lax.all_to_all(projected, "seq", split_axis=0, concat_axis=2, tiled=True)
    qk_local = by_head[:, : 2 * feat_dev]
    values_local = by_head[0, 2 * feat_dev :]
    qk_whole = gathered_copies(qk_local, "fsdp", 0)
    length = qk_whole.shape[2]
    queries = qk_whole[:, :feat_dev].reshape(-1, length)
    key_vectors = qk_whole[:, feat_dev:].reshape(-1, length)
    numerator = attend(queries, key_vectors, values_local)
    out_weights = lax.all_gather(w_out, "seq", axis=0, tiled=True)
    heads_total = out_weights.shape[0]
    head_width = out_weights.shape[1]
    by_token = lax.all_to_all(numerator[None], "seq", split_axis=2, concat_axis=0, tiled=True)
    everyone = gathered_copies(by_token[None], ("fsdp", "sub"), 0)
    arranged = everyone.reshape(
        lax.axis_size("fsdp"),
        lax.axis_size("sub"),
        everyone.shape[1],
        everyone.shape[2],
        everyone.shape[3],
    )
    arranged = jnp.transpose(arranged, (2, 1, 0, 3, 4)).reshape(heads_total, head_width, -1)
    attended = head_norm(arranged, head_gain, 1)
    mixed = jnp.einsum("het,hed->td", attended, out_weights, preferred_element_type=jnp.float32)
    return mixed.astype(jnp.bfloat16)


def solution(mesh):
    in_specs = (
        P(("groups", "seq"), None),
        P(),
        P(("seq", "sub"), "fsdp", None),
        P(("seq", "sub"), "fsdp", None),
        P(("seq", "sub"), "fsdp", None),
        P(),
        P("seq", None, ("fsdp", "sub")),
    )
    out_specs = P(("groups", "seq"), ("fsdp", "sub"))
    return jax.shard_map(
        per_device, mesh=mesh, in_specs=in_specs, out_specs=out_specs, check_vma=False
    )
```

profile of v0, /device:TPU:65, one launch (start us, length us, event | category | flops | bytes accessed | tf_op | source)
XLA Modules:
  0.0 342.6 jit_solution(4627285938782507637)
XLA Ops:
  6.6 1.9 pad_maximum_fusion
  8.5 3.1 fusion.18
  11.7 119.0 %all-gather.3.cloned.1.call-done = bf16[16,20,8192]{2,1,0:T(8,128)(2,1)} async-done(((bf16[1,20,8192]{2,1,0:T(8,128)(2,1)}), bf16[16,20,8192]{2,1,0:T(8,128)(2,1)}) %all-gather.3.cloned.1.call-update) | async-done | bytes 5242896 | tf_op jit(solution)/shard_map/all_gather | solution.py:90
  130.6 6.7 %fusion.45 = bf16[16,20,256]{2,1,0:T(8,128)(2,1)} fusion(bf16[16,20,8192]{2,1,0:T(8,128)(2,1)} %all-gather.3.cloned.1.call-done, bf16[256,8192]{1,0:T(8,128)(2,1)} %param.17, f32[8192]{0:T(1024)S(1)} %copy-done.6, f32[256]{0:T(256)S(1)} %add_rsqrt_fusion), kind=kOutput, calls=%fused_computation.54 | convolution fusion | flops 1350647808 | bytes 9634816 | tf_op jit(solution)/shard_map/hcd,td->hct/dot_general | solution.py:91
  137.3 9.1 %all-to-all-start = ((bf16[16,20,256]{2,1,0:T(8,128)(2,1)}), bf16[16,20,256]{2,1,0:T(8,128)(2,1)S(1)}, u32[]{:S(2)}, u32[]{:S(2)}) async-start(bf16[16,20,256]{2,1,0:T(8,128)(2,1)} %fusion.45), calls=%async_computation | async-start | bytes 393216 | tf_op jit(solution)/shard_map/all_to_all | solution.py:94
  147.3 11.2 %all-to-all-done = bf16[16,20,256]{2,1,0:T(8,128)(2,1)S(1)} async-done(((bf16[16,20,256]{2,1,0:T(8,128)(2,1)}), bf16[16,20,256]{2,1,0:T(8,128)(2,1)S(1)}, u32[]{:S(2)}, u32[]{:S(2)}) %all-to-all-start) | async-done | bytes 163872 | tf_op jit(solution)/shard_map/all_to_all | solution.py:94
  159.4 6.4 %all-to-all-start.1 = ((bf16[8,1,4,4096]{3,2,1,0:T(4,128)(2,1)}), bf16[8,1,4,4096]{3,2,1,0:T(4,128)(2,1)S(1)}, u32[]{:S(2)}, u32[]{:S(2)}) async-start(bf16[8,1,4,4096]{3,2,1,0:T(4,128)(2,1)} %broadcast_in_dim.37), calls=%async_computation.1 | async-start | bytes 524288 | tf_op jit(solution)/shard_map/all_to_all | solution.py:19
  167.3 7.9 %all-to-all-done.1 = bf16[8,1,4,4096]{3,2,1,0:T(4,128)(2,1)S(1)} async-done(((bf16[8,1,4,4096]{3,2,1,0:T(4,128)(2,1)}), bf16[8,1,4,4096]{3,2,1,0:T(4,128)(2,1)S(1)}, u32[]{:S(2)}, u32[]{:S(2)}) %all-to-all-start.1) | async-done | bytes 262176 | tf_op jit(solution)/shard_map/all_to_all | solution.py:19
  175.4 1.4 fusion.62
  176.9 2.5 gather_fusion
  179.3 2.5 gather_fusion.1
  181.9 1.3 gather_fusion.2
  183.2 2.5 gather_fusion.3
  185.7 2.4 multiply_convert_fusion.3
  191.5 1.8 multiply_convert_fusion.2
  195.3 19.3 %while.11 = (s32[]{:T(128)}, f32[8,16,512]{2,1,0:T(8,128)S(1)}, s32[8]{0:T(128)S(1)}, bf16[16,4096]{1,0:T(8,128)(2,1)}, bf16[16,4096]{1,0:T(8,128)(2,1)S(1)}, /*...) while((s32[]{:T(128)}, f32[8,16,512]{2,1,0:T(8,128)S(1)}, ...), condition=%wide.region_2.3_spmd.clone, body=%wide.region_1.0_spmd.clone.sunk | while | flops 18874372 | bytes 84127 | solution.py:79
  196.5 1.2 fusion.81
  198.9 1.2 fusion.81
  201.4 1.2 fusion.81
  203.8 1.2 fusion.81
  206.2 1.2 fusion.81
  208.6 1.2 fusion.81
  211.0 1.2 fusion.81
  213.4 1.2 fusion.81
  215.3 2.7 copy.76
  218.5 22.6 %reduce.4 = bf16[4096,16]{1,0:T(8,128)(2,1)S(1)} reduce(bf16[4096,1,16]{2,1,0:T(2,128)(2,1)S(1)} %bitcast.70, bf16[]{:T(256)} %broadcast.136), dimensions={1}, to_apply=%bitcast.56.reduce_sub_computation | reduce | bytes 262146
  242.3 22.1 %all_to_all.43 = bf16[16,2,2048]{2,1,0:T(2,128)(2,1)S(1)} all-to-all(bf16[16,2,2048]{2,1,0:T(2,128)(2,1)S(1)} %reshape.133), channel_id=1, replica_groups=mesh['groups'=2,'seq'=16,'fsdp'=8,'sub'=2] {'seq'}, dimensions={0} | all-to-all | bytes 262144 | tf_op jit(solution)/shard_map/all_to_all | solution.py:105
  264.4 1.8 reshape.134
  266.2 2.0 copy.77
  268.5 57.5 %all_to_all.44 = bf16[16,1,16,16,256]{4,3,2,1,0:T(8,128)(2,1)S(1)} all-to-all(bf16[16,1,16,16,256]{4,3,2,1,0:T(8,128)(2,1)S(1)} %broadcast_in_dim.43), channel_id=1, replica_groups=mesh['groups'=2,'seq'=16,'fsdp'=8,'sub'=2] {'fsdp','sub'}, dimensions={0} | all-to-all | bytes 4194304 | tf_op jit(solution)/shard_map/all_to_all | solution.py:19
  326.6 2.6 copy.80
  330.2 5.5 %fusion.44 = bf16[256,512]{1,0:T(8,128)(2,1)} fusion(bf16[32,128,512]{2,1,0:T(8,128)(2,1)} %all-gather.5.cloned.1.call-done, f32[32,128,256]{2,1,0:T(8,128)} %bitcast.72, f32[128]{0:T(128)S(1)} %copy-done.7, f32[32,256]{1,0:T(8,128)S(1)} %rsqrt.21), kind=kOutput, calls=%fused_computation.53 | convolution fusion | flops 1077018624 | bytes 8684032 | tf_op jit(solution)/shard_map/het,hed->td/dot_general | solution.py:116
  (75 shorter events, 17.8 us)
Async XLA Ops:
  6.5 124.1 %copy-start.6 = (f32[8192]{0:T(1024)S(1)}, f32[8192]{0:T(1024)}, u32[]{:S(2)}) copy-start(f32[8192]{0:T(1024)} %param.18) | copy-start | bytes 98308
  6.5 124.1 %all-gather.3.cloned.1.call-start = ((), (), s32[]{:S(2)}) async-start(), calls=%async_computation.4 | async-start | bytes 6684672 | tf_op jit(solution)/shard_map/all_gather | solution.py:90
  11.6 135.6 %copy-start.5 = (s32[120]{0:T(128)S(1)}, s32[120]{0:T(128)}, u32[]{:S(2)}) copy-start(s32[120]{0:T(128)} %constant.78) | copy-start | bytes 1444
  11.6 135.6 %copy-start.4 = (s32[120]{0:T(128)S(1)}, s32[120]{0:T(128)}, u32[]{:S(2)}) copy-start(s32[120]{0:T(128)} %constant.79) | copy-start | bytes 1444
  137.3 21.2 %all-to-all-start = ((bf16[16,20,256]{2,1,0:T(8,128)(2,1)}), bf16[16,20,256]{2,1,0:T(8,128)(2,1)S(1)}, u32[]{:S(2)}, u32[]{:S(2)}) async-start(bf16[16,20,256]{2,1,0:T(8,128)(2,1)} %fusion.45), calls=%async_computation | async-start | bytes 393216 | tf_op jit(solution)/shard_map/all_to_all | solution.py:94
  146.4 183.8 %all-gather.5.cloned.1.call-start = ((), (), s32[]{:S(2)}) async-start(), calls=%async_computation.5 | async-start | bytes 4456448 | tf_op jit(solution)/shard_map/all_gather | solution.py:102
  159.4 15.8 %all-to-all-start.1 = ((bf16[8,1,4,4096]{3,2,1,0:T(4,128)(2,1)}), bf16[8,1,4,4096]{3,2,1,0:T(4,128)(2,1)S(1)}, u32[]{:S(2)}, u32[]{:S(2)}) async-start(bf16[8,1,4,4096]{3,2,1,0:T(4,128)(2,1)} %broadcast_in_dim.37), calls=%async_computation.1 | async-start | bytes 524288 | tf_op jit(solution)/shard_map/all_to_all | solution.py:19
  191.5 1.9 copy-start
  193.3 0.9 copy-start.1
  193.3 1.0 copy-start.2
  193.3 1.0 copy-start.3
  194.3 0.9 copy-start.8
  329.2 1.0 copy-start.7
Sparse Core Ops, SparseCore 0:
  9.4 121.1 all-gather.2
  149.3 71.7 all-gather.4
where the time goes:
time: 344 us; the launch traced here: 343 us
  waiting for transfers between devices  139 us (40%)
  blocking collectives  79.6 us (23%)
  other arithmetic  34.7 us (10%)
  local copies, waits for them, and re-layouts  32.1 us (9%)
  matrix products  22.6 us (7%)
  starting transfers between devices  15.6 us (5%)
  between operations  13.8 us (4%)
  loops' own time  5.26 us (2%)
    all_gather x1, waiting for transfers between devices, per_device(): head_weights = lax.all_gather(stacked, 'seq', axis=0, tiled=True)  119 us
    all_to_all x1, blocking collectives, copy_for_each(): return lax.all_to_all(copies, axis, split_axis=0, concat_axis=0, tiled=True)  57.5 us
    unnamed x1, other arithmetic  22.6 us
    all_to_all x1, blocking collectives, per_device(): lax.all_to_all(numerator[None], 'seq', split_axis=2, concat_axis=0, tiled...  22.1 us
    all_to_all x1, waiting for transfers between devices, per_device(): lax.all_to_all(projected, 'seq', split_axis=0, concat_axis=2, tiled=True)  11.2 us
    dot_general x8, matrix products, one_block(): jnp.einsum('ej,jt->et', value_block, weight, preferred_element_type=jnp.f...  9.3 us
    all_to_all x1, starting transfers between devices, per_device(): lax.all_to_all(projected, 'seq', split_axis=0, concat_axis=2, tiled=True)  9.07 us
    gather x4, local copies, waits for them, and re-layouts, taylor_first(): cross_terms = vectors[first_row] * vectors[second_row] / 4.0  8.71 us
  transfers between devices with their start and end apart: 4, of which 3 were waited for; matrix products, arithmetic and copies ran while one was open for 22% of the time, Pallas kernels for 0%

commit v1 on v0

--- a/solution.py
+++ b/solution.py
@@ -87,7 +87,9 @@
     meansq = jnp.mean(inputs * inputs, axis=1, keepdims=True)
     normed = (inputs * lax.rsqrt(meansq + 1e-05) * norm_gain).astype(jnp.bfloat16)
     stacked = jnp.concatenate([w_query, w_key, w_value], 1)
-    head_weights = lax.all_gather(stacked, "seq", axis=0, tiled=True)
+    head_weights = jnp.concatenate(
+        lax.all_to_all(jnp.stack([stacked] * lax.axis_size("seq")), "seq", 0, 0), axis=0
+    )
     projected = jnp.einsum(
         "hcd,td->hct", head_weights, normed, preferred_element_type=jnp.float32
     ).astype(jnp.bfloat16)

time: 344 us -> 543 us (1.58)
  waiting for transfers between devices: 139 us -> 289 us
  starting transfers between devices: 15.6 us -> 62.8 us
    all_to_all x0 -> x1, waiting for transfers between devices: none -> 268 us  [per_device(): lax.all_to_all(jnp.stack([stacked] * lax.axis_size('seq')), 'seq', 0, 0)]
    all_gather x1 -> x0, waiting for transfers between devices: 119 us -> none  [per_device(): head_weights = lax.all_gather(stacked, 'seq', axis=0, tiled=True)]
    all_to_all x0 -> x1, starting transfers between devices: none -> 44.2 us  [per_device(): lax.all_to_all(jnp.stack([stacked] * lax.axis_size('seq')), 'seq', 0, 0)]
  transfers between devices with their start and end apart: 4 -> 4, of which waited for: 3 -> 3; matrix products, arithmetic and copies ran while one was open for 22% -> 14% of each run, Pallas kernels for 0% -> 0%
where the time goes in v1:
time: 543 us; the launch traced here: 542 us
  waiting for transfers between devices  289 us (53%)
  blocking collectives  79.4 us (15%)
  starting transfers between devices  62.8 us (12%)
  local copies, waits for them, and re-layouts  35.5 us (7%)
  other arithmetic  34 us (6%)
  matrix products  22.6 us (4%)
  between operations  13.8 us (3%)
    all_to_all x1, waiting for transfers between devices, per_device(): lax.all_to_all(jnp.stack([stacked] * lax.axis_size('seq')), 'seq', 0, 0)  268 us
    all_to_all x1, blocking collectives, copy_for_each(): return lax.all_to_all(copies, axis, split_axis=0, concat_axis=0, tiled=True)  57.5 us
    all_to_all x1, starting transfers between devices, per_device(): lax.all_to_all(jnp.stack([stacked] * lax.axis_size('seq')), 'seq', 0, 0)  44.2 us
    unnamed x1, other arithmetic  22.6 us
    all_to_all x1, blocking collectives, per_device(): lax.all_to_all(numerator[None], 'seq', split_axis=2, concat_axis=0, tiled...  21.8 us
    all_to_all x1, waiting for transfers between devices, per_device(): lax.all_to_all(projected, 'seq', split_axis=0, concat_axis=2, tiled=True)  11.4 us
    all_to_all x1, starting transfers between devices, per_device(): lax.all_to_all(projected, 'seq', split_axis=0, concat_axis=2, tiled=True)  11.3 us
  transfers between devices with their start and end apart: 4, of which 3 were waited for; matrix products, arithmetic and copies ran while one was open for 14% of the time, Pallas kernels for 0%

profile of v1, /device:TPU:65, one launch (start us, length us, event | category | flops | bytes accessed | tf_op | source)
XLA Modules:
  0.0 541.8 jit_solution(9713140328975303488)
XLA Ops:
  7.7 3.4 stack.2
  11.1 44.2 %all-to-all-start = ((bf16[16,1,20,8192]{3,2,1,0:T(8,128)(2,1)}), bf16[16,1,20,8192]{3,2,1,0:T(8,128)(2,1)}, u32[]{:S(2)}, u32[]{:S(2)}) async-start(bf16[16,1,20,8192]{3,2,1,0:T(8,128)(2,1)} %stack.2), calls=%async_computation | async-start | bytes 12582912 | tf_op jit(solution)/shard_map/all_to_all | solution.py:91
  55.3 3.1 fusion.18
  58.5 268.4 %all-to-all-done = bf16[16,1,20,8192]{3,2,1,0:T(8,128)(2,1)} async-done(((bf16[16,1,20,8192]{3,2,1,0:T(8,128)(2,1)}), bf16[16,1,20,8192]{3,2,1,0:T(8,128)(2,1)}, u32[]{:S(2)}, u32[]{:S(2)}) %all-to-all-start) | async-done | bytes 5242912 | tf_op jit(solution)/shard_map/all_to_all | solution.py:91
  326.9 6.7 %fusion.46 = bf16[16,20,256]{2,1,0:T(8,128)(2,1)} fusion(bf16[256,8192]{1,0:T(8,128)(2,1)} %param.17, f32[8192]{0:T(1024)S(1)} %copy-done.6, f32[256]{0:T(256)S(1)} %add_rsqrt_fusion, bf16[16,1,20,8192]{3,2,1,0:T(8,128)(2,1)} %all-to-all-done), kind=kOutput, calls=%fused_computation.55 | convolution fusion | flops 1350647808 | bytes 9634816 | tf_op jit(solution)/shard_map/hcd,td->hct/dot_general | solution.py:93
  333.6 11.3 %all-to-all-start.1 = ((bf16[16,20,256]{2,1,0:T(8,128)(2,1)}), bf16[16,20,256]{2,1,0:T(8,128)(2,1)S(1)}, u32[]{:S(2)}, u32[]{:S(2)}) async-start(bf16[16,20,256]{2,1,0:T(8,128)(2,1)} %fusion.46), calls=%async_computation.1 | async-start | bytes 393216 | tf_op jit(solution)/shard_map/all_to_all | solution.py:96
  345.8 11.4 %all-to-all-done.1 = bf16[16,20,256]{2,1,0:T(8,128)(2,1)S(1)} async-done(((bf16[16,20,256]{2,1,0:T(8,128)(2,1)}), bf16[16,20,256]{2,1,0:T(8,128)(2,1)S(1)}, u32[]{:S(2)}, u32[]{:S(2)}) %all-to-all-start.1) | async-done | bytes 163872 | tf_op jit(solution)/shard_map/all_to_all | solution.py:96
  358.1 7.2 %all-to-all-start.2 = ((bf16[8,1,4,4096]{3,2,1,0:T(4,128)(2,1)}), bf16[8,1,4,4096]{3,2,1,0:T(4,128)(2,1)S(1)}, u32[]{:S(2)}, u32[]{:S(2)}) async-start(bf16[8,1,4,4096]{3,2,1,0:T(4,128)(2,1)} %broadcast_in_dim.37), calls=%async_computation.2 | async-start | bytes 524288 | tf_op jit(solution)/shard_map/all_to_all | solution.py:19
  366.7 8.0 %all-to-all-done.2 = bf16[8,1,4,4096]{3,2,1,0:T(4,128)(2,1)S(1)} async-done(((bf16[8,1,4,4096]{3,2,1,0:T(4,128)(2,1)}), bf16[8,1,4,4096]{3,2,1,0:T(4,128)(2,1)S(1)}, u32[]{:S(2)}, u32[]{:S(2)}) %all-to-all-start.2) | async-done | bytes 262176 | tf_op jit(solution)/shard_map/all_to_all | solution.py:19
  374.9 1.3 fusion.65
  376.3 2.5 gather_fusion
  378.8 2.5 gather_fusion.1
  381.4 1.3 gather_fusion.2
  382.7 2.5 gather_fusion.3
  385.1 2.4 multiply_convert_fusion.3
  391.0 1.8 multiply_convert_fusion.2
  394.8 19.3 %while.11 = (s32[]{:T(128)}, f32[8,16,512]{2,1,0:T(8,128)S(1)}, s32[8]{0:T(128)S(1)}, bf16[16,4096]{1,0:T(8,128)(2,1)}, bf16[16,4096]{1,0:T(8,128)(2,1)S(1)}, /*...) while((s32[]{:T(128)}, f32[8,16,512]{2,1,0:T(8,128)S(1)}, ...), condition=%wide.region_2.3_spmd.clone, body=%wide.region_1.0_spmd.clone.sunk | while | flops 18874372 | bytes 84127 | solution.py:79
  396.0 1.2 fusion.83
  398.4 1.2 fusion.83
  400.8 1.2 fusion.83
  405.6 1.2 fusion.83
  408.1 1.2 fusion.83
  410.5 1.2 fusion.83
  412.9 1.2 fusion.83
  414.8 2.7 copy.76
  418.0 22.6 %reduce.4 = bf16[4096,16]{1,0:T(8,128)(2,1)S(1)} reduce(bf16[4096,1,16]{2,1,0:T(2,128)(2,1)S(1)} %bitcast.76, bf16[]{:T(256)} %broadcast.139), dimensions={1}, to_apply=%bitcast.63.reduce_sub_computation | reduce | bytes 262146
  441.8 21.8 %all_to_all.48 = bf16[16,2,2048]{2,1,0:T(2,128)(2,1)S(1)} all-to-all(bf16[16,2,2048]{2,1,0:T(2,128)(2,1)S(1)} %reshape.140), channel_id=1, replica_groups=mesh['groups'=2,'seq'=16,'fsdp'=8,'sub'=2] {'seq'}, dimensions={0} | all-to-all | bytes 262144 | tf_op jit(solution)/shard_map/all_to_all | solution.py:107
  463.6 1.8 reshape.141
  465.4 2.0 copy.77
  467.7 57.5 %all_to_all.49 = bf16[16,1,16,16,256]{4,3,2,1,0:T(8,128)(2,1)S(1)} all-to-all(bf16[16,1,16,16,256]{4,3,2,1,0:T(8,128)(2,1)S(1)} %broadcast_in_dim.43), channel_id=1, replica_groups=mesh['groups'=2,'seq'=16,'fsdp'=8,'sub'=2] {'fsdp','sub'}, dimensions={0} | all-to-all | bytes 4194304 | tf_op jit(solution)/shard_map/all_to_all | solution.py:19
  525.8 2.6 copy.80
  529.5 5.5 %fusion.45 = bf16[256,512]{1,0:T(8,128)(2,1)} fusion(bf16[32,128,512]{2,1,0:T(8,128)(2,1)} %all-gather.2.cloned.1.call-done, f32[32,128,256]{2,1,0:T(8,128)} %bitcast.78, f32[128]{0:T(128)S(1)} %copy-done.7, f32[32,256]{1,0:T(8,128)S(1)} %rsqrt.21), kind=kOutput, calls=%fused_computation.54 | convolution fusion | flops 1077018624 | bytes 8684032 | tf_op jit(solution)/shard_map/het,hed->td/dot_general | solution.py:118
  (75 shorter events, 20.0 us)
Async XLA Ops:
  11.1 315.8 %all-to-all-start = ((bf16[16,1,20,8192]{3,2,1,0:T(8,128)(2,1)}), bf16[16,1,20,8192]{3,2,1,0:T(8,128)(2,1)}, u32[]{:S(2)}, u32[]{:S(2)}) async-start(bf16[16,1,20,8192]{3,2,1,0:T(8,128)(2,1)} %stack.2), calls=%async_computation | async-start | bytes 12582912 | tf_op jit(solution)/shard_map/all_to_all | solution.py:91
  55.3 271.6 %copy-start.6 = (f32[8192]{0:T(1024)S(1)}, f32[8192]{0:T(1024)}, u32[]{:S(2)}) copy-start(f32[8192]{0:T(1024)} %param.18) | copy-start | bytes 98308
  58.4 287.3 %copy-start.5 = (s32[120]{0:T(128)S(1)}, s32[120]{0:T(128)}, u32[]{:S(2)}) copy-start(s32[120]{0:T(128)} %constant.78) | copy-start | bytes 1444
  58.5 287.3 %copy-start.4 = (s32[120]{0:T(128)S(1)}, s32[120]{0:T(128)}, u32[]{:S(2)}) copy-start(s32[120]{0:T(128)} %constant.79) | copy-start | bytes 1444
  333.6 23.6 %all-to-all-start.1 = ((bf16[16,20,256]{2,1,0:T(8,128)(2,1)}), bf16[16,20,256]{2,1,0:T(8,128)(2,1)S(1)}, u32[]{:S(2)}, u32[]{:S(2)}) async-start(bf16[16,20,256]{2,1,0:T(8,128)(2,1)} %fusion.46), calls=%async_computation.1 | async-start | bytes 393216 | tf_op jit(solution)/shard_map/all_to_all | solution.py:96
  344.9 184.6 %all-gather.2.cloned.1.call-start = ((), (), s32[]{:S(2)}) async-start(), calls=%async_computation.5 | async-start | bytes 4456448 | tf_op jit(solution)/shard_map/all_gather | solution.py:104
  358.1 16.5 %all-to-all-start.2 = ((bf16[8,1,4,4096]{3,2,1,0:T(4,128)(2,1)}), bf16[8,1,4,4096]{3,2,1,0:T(4,128)(2,1)S(1)}, u32[]{:S(2)}, u32[]{:S(2)}) async-start(bf16[8,1,4,4096]{3,2,1,0:T(4,128)(2,1)} %broadcast_in_dim.37), calls=%async_computation.2 | async-start | bytes 524288 | tf_op jit(solution)/shard_map/all_to_all | solution.py:19
  391.0 1.9 copy-start
  392.8 0.9 copy-start.1
  392.8 1.0 copy-start.2
  392.8 1.0 copy-start.3
  393.8 1.0 copy-start.8
  528.4 1.0 copy-start.7
Sparse Core Ops, SparseCore 0:
  347.8 73.5 all-gather.1
